TPU v7x, 32 devices: a whole 2x2x4 slice. The times are simulated.
32 devices in a mesh: row: 4 (over z), col: 8 (over y, x, core).
Axes of the slice: x: 2, y: 2, z: 4, core: 2. Of those that a mesh axis runs over, the one named last changes fastest.
Arguments:
- tile_data: bfloat16 [8, 4, 8, 2, 128, 128], P(None, 'row', 'col'), may hold values from 0 to 1, as said below
- tile_cols: int32 [8, 4, 8, 2], P(None, 'row', 'col'), may hold values from -1 to 31, as said below
Outputs:
- vertex_triangles: float32 [8, 4, 128], P(None, 'row', 'col')
- triangles: float32 [], replicated
Inputs may be any that keep to these rules, and one draw needn't show every extreme that they name: `tile_cols`: slot (a, r, c, s) holds -1 (empty) or a tile column J with J % 8 == c and J >= a 4 + r; the columns of one tile row are distinct; every slot of tile row 0 is filled; tile row I keeps each slot that has an allowed column with probability (32 - I) / 32, so rows with a lower index hold more tiles on average. `tile_data`: entries are 0 or 1; tiles of empty slots are zero; a tile whose column equals its tile row is strictly upper triangular; about one entry in 8 of a stored tile is 1, with edges clustered among groups of vertices.
All inputs are finite; a program needn't handle non-finite values.
Results may differ from a plain program's by a relative error of at most 0.0003.
Values may be sent and summed in bfloat16 or wider, within the bound.
A program may use at most 128 MiB of HBM per device.

v0:
```python
import jax
import jax.numpy as jnp
from jax import lax
from jax.sharding import PartitionSpec as P

vertex_scale = 2.0 ** (-14)
total_scale = 2.0 ** (-12)


def taken_in(share, axis, dim):

    def gathered(part):
        return lax.all_gather(part, axis, axis=dim, tiled=True)

    return jax.tree.map(gathered, share)


def tile_counts(stored, middle, own_tiles, own_cols, col_tiles, col_index):
    valid = middle >= 0
    clipped = jnp.clip(middle, 0, col_tiles.shape[0] - 1).astype(jnp.int32)
    partner = col_tiles[clipped]
    partner_cols = col_index[clipped]
    matches = partner_cols[:, :, None] == own_cols[None, None, :]
    matches = matches & valid[:, None, None] & (own_cols >= 0)[None, None, :]
    weights = matches.astype(jnp.bfloat16)
    targets = jnp.einsum("pqs,sxz->pqxz", weights, own_tiles, preferred_element_type=jnp.float32)
    paths = jnp.einsum("pxy,pqyz->pqxz", stored, partner, preferred_element_type=jnp.float32)
    return jnp.sum(paths * targets, axis=(0, 1, 3))


def on_device(tile_data, tile_cols):
    rows_here = tile_data.shape[0]
    slots = tile_data.shape[3]
    width = tile_data.shape[4]
    own_tiles = tile_data[:, 0, 0]
    own_cols = tile_cols[:, 0, 0]
    row_index = lax.all_gather(tile_cols, "col", axis=2, tiled=True)
    col_index = lax.all_gather(tile_cols, "row", axis=1, tiled=True)
    col_tiles = lax.all_gather(tile_data, "row", axis=1, tiled=True)
    tile_rows = col_index.shape[0] * col_index.shape[1]
    col_index = col_index.reshape(tile_rows, slots)
    col_tiles = col_tiles.reshape(tile_rows, slots, width, width)

    def add_piece(carry, piece, start):
        devices_here = piece.shape[2]
        middle = lax.dynamic_slice_in_dim(row_index, start.astype(jnp.int32), devices_here, 2)
        middle = middle.reshape(rows_here, devices_here * slots)
        stored = piece.reshape(rows_here, devices_here * slots, width, width)

        def per_row(packed):
            return tile_counts(packed[0], packed[1], packed[2], packed[3], col_tiles, col_index)

        return carry + lax.map(per_row, (stored, middle, own_tiles, own_cols))

    initial = jnp.zeros((rows_here, width), jnp.float32)
    partial_value = add_piece(initial, taken_in(tile_data, "col", 2), jnp.int32(0))
    shares = lax.psum_scatter(
        partial_value.reshape(rows_here, 1, width), "col", scatter_dimension=2, tiled=True
    )
    vertices = tile_rows * width
    overall = lax.psum(jnp.sum(partial_value), ("row", "col"))
    return (shares * vertex_scale, overall * (total_scale / vertices))


def solution(mesh):
    return jax.shard_map(
        on_device,
        mesh=mesh,
        in_specs=(P(None, "row", "col", None, None, None), P(None, "row", "col", None)),
        out_specs=(P(None, "row", "col"), P()),
        check_vma=False,
    )
```

profile of v0, /device:TPU:0, one launch (start us, length us, event | category | flops | bytes accessed | tf_op | source)
XLA Modules:
  0.0 213.6 jit_solution(9713125407251959521)
XLA Ops:
  7.2 0.7 all-gather.3.cloned.1.call-update
  8.0 0.7 all-gather.5.cloned.1.call-update
  8.7 2.4 %copy.37 = bf16[8,1,1,2,128,128]{5,3,4,0,2,1:T(2,128)(2,1)} copy(bf16[8,1,1,2,128,128]{5,4,3,2,1,0:T(8,128)(2,1)} %param.4) | data formatting | bytes 1048576 | tf_op args[0]
  11.1 12.6 %all_gather.15 = s32[8,4,1,2]{0,3,2,1:T(2,128)S(1)} all-gather(s32[8,1,1,2]{0,3,2,1:T(2,128)S(1)} %copy-done.1), channel_id=1, replica_groups=mesh['row'=4,'col'=8] {'row'}, dimensions={1}, use_global_device_ids=true | all-gather | bytes 320 | tf_op jit(solution)/shard_map/all_gather | solution.py:38
  23.8 0.1 copy.32
  23.9 8.9 %all_gather.12 = s32[8,1,8,2]{0,3,1,2:T(2,128)S(1)} all-gather(s32[8,1,1,2]{0,3,1,2:T(2,128)S(1)} %bitcast.68), channel_id=1, replica_groups=mesh['row'=4,'col'=8] {'col'}, dimensions={2}, use_global_device_ids=true | all-gather | bytes 576 | tf_op jit(solution)/shard_map/all_gather | solution.py:37
  33.0 25.0 %all-gather.3.cloned.1.call-done = bf16[8,4,1,2,128,128]{5,4,3,2,1,0:T(8,128)(2,1)} async-done(((bf16[8,1,1,2,128,128]{5,4,3,2,1,0:T(8,128)(2,1)}), bf16[8,4,1,2,128,128]{5,4,3,2,1,0:T(8,128)(2,1)}) %all-gather.3.cloned.1.call-update) | async-done | bytes 2097168 | tf_op jit(solution)/shard_map/all_gather | solution.py:39
  58.0 37.3 %all-gather.5.cloned.1.call-done = bf16[8,1,8,2,128,128]{5,4,3,2,1,0:T(8,128)(2,1)} async-done(((bf16[8,1,1,2,128,128]{5,4,3,2,1,0:T(8,128)(2,1)}), bf16[8,1,8,2,128,128]{5,4,3,2,1,0:T(8,128)(2,1)}) %all-gather.5.cloned.1.call-update) | async-done | bytes 4194320 | tf_op jit(solution)/shard_map/all_gather | solution.py:13
  95.3 67.3 %while.10 = (s32[]{:T(128)}, f32[8,128]{1,0:T(8,128)S(1)}, s32[8,16]{1,0:T(8,128)S(1)}, bf16[32,2,128,128]{3,2,1,0:T(8,128)(2,1)}, bf16[8,16,128,128]{3,2,1,0:T(...) while((s32[]{:T(128)}, f32[8,128]{1,0:T(8,128)S(1)}, ...), condition=%wide.region_2.3_spmd, body=%wide.region_0.2_spmd.sunk | while | flops 137364624 | bytes 20520652 | solution.py:53
  95.3 0.6 gather_fusion
  95.9 0.1 copy.40
  96.0 1.4 fusion.32
  97.4 1.8 copy.41
  99.3 2.5 %gather_fusion.1 = bf16[16,2,128,128]{3,2,1,0:T(8,128)(2,1)S(1)} fusion(bf16[32,2,128,128]{3,2,1,0:T(8,128)(2,1)} %get-tuple-element.163, s32[1024]{0:T(1024)S(1)} %pad_clamp_fusion.2), kind=kCustom, calls=%fused_computation.clone.1 | custom fusion | bytes 2097216 | tf_op jit(solution)/shard_map/while/body/eval_jaxpr/gather | solution.py:21
  101.8 1.9 fusion.33
  103.7 0.6 gather_fusion
  104.3 0.1 copy.40
  104.4 1.4 fusion.32
  105.8 1.8 copy.41
  107.7 2.5 %gather_fusion.1 = bf16[16,2,128,128]{3,2,1,0:T(8,128)(2,1)S(1)} fusion(bf16[32,2,128,128]{3,2,1,0:T(8,128)(2,1)} %get-tuple-element.163, s32[1024]{0:T(1024)S(1)} %pad_clamp_fusion.2), kind=kCustom, calls=%fused_computation.clone.1 | custom fusion | bytes 2097216 | tf_op jit(solution)/shard_map/while/body/eval_jaxpr/gather | solution.py:21
  110.2 1.9 fusion.33
  112.1 0.6 gather_fusion
  112.7 0.1 copy.40
  112.8 1.4 fusion.32
  114.3 1.8 copy.41
  116.1 2.5 %gather_fusion.1 = bf16[16,2,128,128]{3,2,1,0:T(8,128)(2,1)S(1)} fusion(bf16[32,2,128,128]{3,2,1,0:T(8,128)(2,1)} %get-tuple-element.163, s32[1024]{0:T(1024)S(1)} %pad_clamp_fusion.2), kind=kCustom, calls=%fused_computation.clone.1 | custom fusion | bytes 2097216 | tf_op jit(solution)/shard_map/while/body/eval_jaxpr/gather | solution.py:21
  118.6 1.9 fusion.33
  120.5 0.6 gather_fusion
  121.1 0.1 copy.40
  121.2 1.4 fusion.32
  122.7 1.8 copy.41
  124.5 2.5 %gather_fusion.1 = bf16[16,2,128,128]{3,2,1,0:T(8,128)(2,1)S(1)} fusion(bf16[32,2,128,128]{3,2,1,0:T(8,128)(2,1)} %get-tuple-element.163, s32[1024]{0:T(1024)S(1)} %pad_clamp_fusion.2), kind=kCustom, calls=%fused_computation.clone.1 | custom fusion | bytes 2097216 | tf_op jit(solution)/shard_map/while/body/eval_jaxpr/gather | solution.py:21
  127.0 1.9 fusion.33
  129.0 0.6 gather_fusion
  129.5 0.1 copy.40
  129.6 1.4 fusion.32
  131.1 1.8 copy.41
  132.9 2.5 %gather_fusion.1 = bf16[16,2,128,128]{3,2,1,0:T(8,128)(2,1)S(1)} fusion(bf16[32,2,128,128]{3,2,1,0:T(8,128)(2,1)} %get-tuple-element.163, s32[1024]{0:T(1024)S(1)} %pad_clamp_fusion.2), kind=kCustom, calls=%fused_computation.clone.1 | custom fusion | bytes 2097216 | tf_op jit(solution)/shard_map/while/body/eval_jaxpr/gather | solution.py:21
  135.4 1.9 fusion.33
  137.4 0.6 gather_fusion
  137.9 0.1 copy.40
  138.0 1.4 fusion.32
  139.5 1.8 copy.41
  141.3 2.5 %gather_fusion.1 = bf16[16,2,128,128]{3,2,1,0:T(8,128)(2,1)S(1)} fusion(bf16[32,2,128,128]{3,2,1,0:T(8,128)(2,1)} %get-tuple-element.163, s32[1024]{0:T(1024)S(1)} %pad_clamp_fusion.2), kind=kCustom, calls=%fused_computation.clone.1 | custom fusion | bytes 2097216 | tf_op jit(solution)/shard_map/while/body/eval_jaxpr/gather | solution.py:21
  143.8 1.9 fusion.33
  145.8 0.6 gather_fusion
  146.3 0.1 copy.40
  146.4 1.4 fusion.32
  147.9 1.8 copy.41
  149.7 2.5 %gather_fusion.1 = bf16[16,2,128,128]{3,2,1,0:T(8,128)(2,1)S(1)} fusion(bf16[32,2,128,128]{3,2,1,0:T(8,128)(2,1)} %get-tuple-element.163, s32[1024]{0:T(1024)S(1)} %pad_clamp_fusion.2), kind=kCustom, calls=%fused_computation.clone.1 | custom fusion | bytes 2097216 | tf_op jit(solution)/shard_map/while/body/eval_jaxpr/gather | solution.py:21
  152.2 1.9 fusion.33
  154.2 0.6 gather_fusion
  154.8 0.1 copy.40
  154.9 1.4 fusion.32
  156.3 1.8 copy.41
  158.2 2.5 %gather_fusion.1 = bf16[16,2,128,128]{3,2,1,0:T(8,128)(2,1)S(1)} fusion(bf16[32,2,128,128]{3,2,1,0:T(8,128)(2,1)} %get-tuple-element.163, s32[1024]{0:T(1024)S(1)} %pad_clamp_fusion.2), kind=kCustom, calls=%fused_computation.clone.1 | custom fusion | bytes 2097216 | tf_op jit(solution)/shard_map/while/body/eval_jaxpr/gather | solution.py:21
  160.7 1.9 fusion.33
  162.6 0.3 copy.33
  162.8 0.8 bitcast_reduce_fusion
  163.7 0.6 reduce_sum.18
  164.3 39.5 %psum.7 = f32[]{:T(128)} all-reduce(f32[]{:T(128)} %reduce_sum.18), channel_id=1, replica_groups=mesh['row'=4,'col'=8] {'row','col'}, use_global_device_ids=true, to_apply=%region_5.6 | all-reduce | flops 1 | bytes 8 | tf_op jit(solution)/shard_map/psum | solution.py:61
  204.4 0.8 reshape_bitcast_fusion
  205.2 0.1 copy.34
  205.3 0.6 broadcast_multiply_fusion
  (66 shorter events, 0.9 us)
Async XLA Ops:
  7.2 4.0 %copy-start.1 = (s32[8,1,1,2]{0,3,2,1:T(2,128)S(1)}, s32[8,1,1,2]{0,3,2,1:T(2,128)}, u32[]{:S(2)}) copy-start(s32[8,1,1,2]{0,3,2,1:T(2,128)} %param.5) | copy-start | bytes 196
  7.2 50.8 %all-gather.3.cloned.1.call-start = ((), (), s32[]{:S(2)}) async-start(), calls=%async_computation.1 | async-start | bytes 2621440 | tf_op jit(solution)/shard_map/all_gather | solution.py:39
  7.9 87.4 %all-gather.5.cloned.1.call-start = ((), (), s32[]{:S(2)}) async-start(), calls=%async_computation.2 | async-start | bytes 4718592 | tf_op jit(solution)/shard_map/all_gather | solution.py:13
  8.7 195.8 %reduce-scatter.4.cloned.1.call-start = ((), (), s32[]{:S(2)}) async-start(), calls=%async_computation.3 | async-start | bytes 73728
  99.3 2.5 %copy-start = (f32[16,2,128,128]{2,3,1,0:T(8,128)S(1)}, f32[16,2,128,128]{2,3,1,0:T(8,128)}, u32[]{:S(2)}) copy-start(f32[16,2,128,128]{2,3,1,0:T(8,128)} %copy.41) | copy-start | bytes 6291460 | tf_op jit(solution)/shard_map/while
  107.7 2.5 %copy-start = (f32[16,2,128,128]{2,3,1,0:T(8,128)S(1)}, f32[16,2,128,128]{2,3,1,0:T(8,128)}, u32[]{:S(2)}) copy-start(f32[16,2,128,128]{2,3,1,0:T(8,128)} %copy.41) | copy-start | bytes 6291460 | tf_op jit(solution)/shard_map/while
  116.1 2.5 %copy-start = (f32[16,2,128,128]{2,3,1,0:T(8,128)S(1)}, f32[16,2,128,128]{2,3,1,0:T(8,128)}, u32[]{:S(2)}) copy-start(f32[16,2,128,128]{2,3,1,0:T(8,128)} %copy.41) | copy-start | bytes 6291460 | tf_op jit(solution)/shard_map/while
  124.5 2.5 %copy-start = (f32[16,2,128,128]{2,3,1,0:T(8,128)S(1)}, f32[16,2,128,128]{2,3,1,0:T(8,128)}, u32[]{:S(2)}) copy-start(f32[16,2,128,128]{2,3,1,0:T(8,128)} %copy.41) | copy-start | bytes 6291460 | tf_op jit(solution)/shard_map/while
  132.9 2.5 %copy-start = (f32[16,2,128,128]{2,3,1,0:T(8,128)S(1)}, f32[16,2,128,128]{2,3,1,0:T(8,128)}, u32[]{:S(2)}) copy-start(f32[16,2,128,128]{2,3,1,0:T(8,128)} %copy.41) | copy-start | bytes 6291460 | tf_op jit(solution)/shard_map/while
  141.3 2.5 %copy-start = (f32[16,2,128,128]{2,3,1,0:T(8,128)S(1)}, f32[16,2,128,128]{2,3,1,0:T(8,128)}, u32[]{:S(2)}) copy-start(f32[16,2,128,128]{2,3,1,0:T(8,128)} %copy.41) | copy-start | bytes 6291460 | tf_op jit(solution)/shard_map/while
  149.7 2.5 %copy-start = (f32[16,2,128,128]{2,3,1,0:T(8,128)S(1)}, f32[16,2,128,128]{2,3,1,0:T(8,128)}, u32[]{:S(2)}) copy-start(f32[16,2,128,128]{2,3,1,0:T(8,128)} %copy.41) | copy-start | bytes 6291460 | tf_op jit(solution)/shard_map/while
  158.2 2.5 %copy-start = (f32[16,2,128,128]{2,3,1,0:T(8,128)S(1)}, f32[16,2,128,128]{2,3,1,0:T(8,128)}, u32[]{:S(2)}) copy-start(f32[16,2,128,128]{2,3,1,0:T(8,128)} %copy.41) | copy-start | bytes 6291460 | tf_op jit(solution)/shard_map/while
Sparse Core Ops, SparseCore 0:
  9.6 48.3 all-gather.2
  59.9 35.3 all-gather.4
  163.8 33.5 reduce-scatter.3
where the time goes:
time: 215 us; the launch traced here: 214 us
  waiting for transfers between devices  63.7 us (30%)
  blocking collectives  61 us (28%)
  local copies, waits for them, and re-layouts  44.8 us (21%)
  matrix products  26.4 us (12%)
  between operations  15.6 us (7%)
    psum x1, blocking collectives, on_device(): overall = lax.psum(jnp.sum(partial_value), ('row', 'col'))  39.5 us
    all_gather x1, waiting for transfers between devices, gathered(): return lax.all_gather(part, axis, axis=dim, tiled=True)  37.3 us
    all_gather x1, waiting for transfers between devices, on_device(): col_tiles = lax.all_gather(tile_data, 'row', axis=1, tiled=True)  25 us
    gather x8, local copies, waits for them, and re-layouts, tile_counts(): partner = col_tiles[clipped]  19.9 us
    dot_general x8, matrix products, tile_counts(): jnp.einsum('pxy,pqyz->pqxz', stored, partner, preferred_element_type=jnp....  14.9 us
    dot_general x8, local copies, waits for them, and re-layouts, tile_counts(): jnp.einsum('pqs,sxz->pqxz', weights, own_tiles, preferred_element_type=jn...  14.7 us
    all_gather x1, blocking collectives, on_device(): col_index = lax.all_gather(tile_cols, 'row', axis=1, tiled=True)  12.6 us
    dot_general x8, matrix products, tile_counts(): jnp.einsum('pqs,sxz->pqxz', weights, own_tiles, preferred_element_type=jn...  11.5 us
  transfers between devices with their start and end apart: 3, of which 2 were waited for; matrix products, arithmetic and copies ran while one was open for 2% of the time, Pallas kernels for 0%

commit v1 on v0

--- a/solution.py
+++ b/solution.py
@@ -35,7 +35,8 @@
     own_tiles = tile_data[:, 0, 0]
     own_cols = tile_cols[:, 0, 0]
     row_index = lax.all_gather(tile_cols, "col", axis=2, tiled=True)
-    col_index = lax.all_gather(tile_cols, "row", axis=1, tiled=True)
+    repeated = jnp.stack([tile_cols] * lax.axis_size("row"))
+    col_index = jnp.concatenate(lax.all_to_all(repeated, "row", 0, 0), axis=1)
     col_tiles = lax.all_gather(tile_data, "row", axis=1, tiled=True)
     tile_rows = col_index.shape[0] * col_index.shape[1]
     col_index = col_index.reshape(tile_rows, slots)

time: 215 us -> 215 us (level)
  blocking collectives: 61 us -> 48.4 us
  starting transfers between devices: 0.11 us -> 6.42 us
  waiting for transfers between devices: 63.7 us -> 68.1 us
    all_gather x1 -> x0, blocking collectives: 12.6 us -> none  [on_device(): col_index = lax.all_gather(tile_cols, 'row', axis=1, tiled=True)]
    all_to_all x0 -> x1, starting transfers between devices: none -> 6.35 us  [on_device(): col_index = jnp.concatenate(lax.all_to_all(repeated, 'row', 0, 0), axis=1)]
    all_gather x1, waiting for transfers between devices: 25 us -> 29.4 us  [on_device(): col_tiles = lax.all_gather(tile_data, 'row', axis=1, tiled=True)]
  transfers between devices with their start and end apart: 3 -> 4, of which waited for: 2 -> 2; matrix products, arithmetic and copies ran while one was open for 2% -> 2% of each run, Pallas kernels for 0% -> 0%
where the time goes in v1:
time: 215 us; the launch traced here: 214 us
  waiting for transfers between devices  68.1 us (32%)
  blocking collectives  48.4 us (23%)
  local copies, waits for them, and re-layouts  46.7 us (22%)
  matrix products  26.4 us (12%)
  between operations  15.6 us (7%)
  starting transfers between devices  6.42 us (3%)
    psum x1, blocking collectives, on_device(): overall = lax.psum(jnp.sum(partial_value), ('row', 'col'))  39.5 us
    all_gather x1, waiting for transfers between devices, gathered(): return lax.all_gather(part, axis, axis=dim, tiled=True)  37.3 us
    all_gather x1, waiting for transfers between devices, on_device(): col_tiles = lax.all_gather(tile_data, 'row', axis=1, tiled=True)  29.4 us
    gather x8, local copies, waits for them, and re-layouts, tile_counts(): partner = col_tiles[clipped]  19.9 us
    dot_general x8, matrix products, tile_counts(): jnp.einsum('pxy,pqyz->pqxz', stored, partner, preferred_element_type=jnp....  14.9 us
    dot_general x8, local copies, waits for them, and re-layouts, tile_counts(): jnp.einsum('pqs,sxz->pqxz', weights, own_tiles, preferred_element_type=jn...  14.8 us
    dot_general x8, matrix products, tile_counts(): jnp.einsum('pqs,sxz->pqxz', weights, own_tiles, preferred_element_type=jn...  11.5 us
    all_gather x1, blocking collectives, on_device(): row_index = lax.all_gather(tile_cols, 'col', axis=2, tiled=True)  8.92 us
  transfers between devices with their start and end apart: 4, of which 2 were waited for; matrix products, arithmetic and copies ran while one was open for 2% of the time, Pallas kernels for 0%

profile of v1, /device:TPU:0, one launch (start us, length us, event | category | flops | bytes accessed | tf_op | source)
XLA Modules:
  0.0 213.6 jit_solution(8520755365105920007)
XLA Ops:
  7.2 0.7 all-gather.3.cloned.1.call-update
  8.0 0.7 all-gather.5.cloned.1.call-update
  8.7 1.3 stack.2
  9.9 6.3 %all-to-all-start = ((s32[4,8,1,1,2]{1,4,3,2,0:T(2,128)}), s32[4,8,1,1,2]{1,4,3,2,0:T(2,128)S(1)}, u32[]{:S(2)}, u32[]{:S(2)}) async-start(s32[4,8,1,1,2]{1,4,3,2,0:T(2,128)} %stack.2), calls=%async_computation | async-start | bytes 8192 | tf_op jit(solution)/shard_map/all_to_all | solution.py:39
  16.3 0.8 copy.26
  17.0 2.4 %copy.35 = bf16[8,1,1,2,128,128]{5,3,4,0,2,1:T(2,128)(2,1)} copy(bf16[8,1,1,2,128,128]{5,4,3,2,1,0:T(8,128)(2,1)} %param.4) | data formatting | bytes 1048576 | tf_op args[0]
  19.5 8.9 %all_gather.9 = s32[8,1,8,2]{0,3,1,2:T(2,128)S(1)} all-gather(s32[8,1,1,2]{0,3,1,2:T(2,128)S(1)} %bitcast.72), channel_id=1, replica_groups=mesh['row'=4,'col'=8] {'col'}, dimensions={2}, use_global_device_ids=true | all-gather | bytes 576 | tf_op jit(solution)/shard_map/all_gather | solution.py:37
  28.5 0.1 copy.30
  28.6 29.4 %all-gather.3.cloned.1.call-done = bf16[8,4,1,2,128,128]{5,4,3,2,1,0:T(8,128)(2,1)} async-done(((bf16[8,1,1,2,128,128]{5,4,3,2,1,0:T(8,128)(2,1)}), bf16[8,4,1,2,128,128]{5,4,3,2,1,0:T(8,128)(2,1)}) %all-gather.3.cloned.1.call-update) | async-done | bytes 2097168 | tf_op jit(solution)/shard_map/all_gather | solution.py:40
  58.0 37.3 %all-gather.5.cloned.1.call-done = bf16[8,1,8,2,128,128]{5,4,3,2,1,0:T(8,128)(2,1)} async-done(((bf16[8,1,1,2,128,128]{5,4,3,2,1,0:T(8,128)(2,1)}), bf16[8,1,8,2,128,128]{5,4,3,2,1,0:T(8,128)(2,1)}) %all-gather.5.cloned.1.call-update) | async-done | bytes 4194320 | tf_op jit(solution)/shard_map/all_gather | solution.py:13
  95.3 67.3 %while.10 = (s32[]{:T(128)}, f32[8,128]{1,0:T(8,128)S(1)}, s32[8,16]{1,0:T(8,128)S(1)}, bf16[32,2,128,128]{3,2,1,0:T(8,128)(2,1)}, bf16[8,16,128,128]{3,2,1,0:T(...) while((s32[]{:T(128)}, f32[8,128]{1,0:T(8,128)S(1)}, ...), condition=%wide.region_2.3_spmd, body=%wide.region_0.2_spmd.sunk | while | flops 137364624 | bytes 20520652 | solution.py:54
  95.3 0.6 gather_fusion
  95.9 0.1 copy.38
  96.0 1.4 fusion.32
  97.4 1.8 copy.39
  99.3 2.5 %gather_fusion.1 = bf16[16,2,128,128]{3,2,1,0:T(8,128)(2,1)S(1)} fusion(bf16[32,2,128,128]{3,2,1,0:T(8,128)(2,1)} %get-tuple-element.163, s32[1024]{0:T(1024)S(1)} %pad_clamp_fusion.2), kind=kCustom, calls=%fused_computation.clone.1 | custom fusion | bytes 2097216 | tf_op jit(solution)/shard_map/while/body/eval_jaxpr/gather | solution.py:21
  101.8 1.9 fusion.33
  103.7 0.6 gather_fusion
  104.3 0.1 copy.38
  104.4 1.4 fusion.32
  105.9 1.8 copy.39
  107.7 2.5 %gather_fusion.1 = bf16[16,2,128,128]{3,2,1,0:T(8,128)(2,1)S(1)} fusion(bf16[32,2,128,128]{3,2,1,0:T(8,128)(2,1)} %get-tuple-element.163, s32[1024]{0:T(1024)S(1)} %pad_clamp_fusion.2), kind=kCustom, calls=%fused_computation.clone.1 | custom fusion | bytes 2097216 | tf_op jit(solution)/shard_map/while/body/eval_jaxpr/gather | solution.py:21
  110.2 1.9 fusion.33
  112.1 0.6 gather_fusion
  112.7 0.1 copy.38
  112.8 1.4 fusion.32
  114.3 1.8 copy.39
  116.1 2.5 %gather_fusion.1 = bf16[16,2,128,128]{3,2,1,0:T(8,128)(2,1)S(1)} fusion(bf16[32,2,128,128]{3,2,1,0:T(8,128)(2,1)} %get-tuple-element.163, s32[1024]{0:T(1024)S(1)} %pad_clamp_fusion.2), kind=kCustom, calls=%fused_computation.clone.1 | custom fusion | bytes 2097216 | tf_op jit(solution)/shard_map/while/body/eval_jaxpr/gather | solution.py:21
  118.6 1.9 fusion.33
  120.6 0.6 gather_fusion
  121.1 0.1 copy.38
  121.2 1.4 fusion.32
  122.7 1.8 copy.39
  124.5 2.5 %gather_fusion.1 = bf16[16,2,128,128]{3,2,1,0:T(8,128)(2,1)S(1)} fusion(bf16[32,2,128,128]{3,2,1,0:T(8,128)(2,1)} %get-tuple-element.163, s32[1024]{0:T(1024)S(1)} %pad_clamp_fusion.2), kind=kCustom, calls=%fused_computation.clone.1 | custom fusion | bytes 2097216 | tf_op jit(solution)/shard_map/while/body/eval_jaxpr/gather | solution.py:21
  127.0 1.9 fusion.33
  129.0 0.6 gather_fusion
  129.6 1.4 fusion.32
  131.1 1.8 copy.39
  132.9 2.5 %gather_fusion.1 = bf16[16,2,128,128]{3,2,1,0:T(8,128)(2,1)S(1)} fusion(bf16[32,2,128,128]{3,2,1,0:T(8,128)(2,1)} %get-tuple-element.163, s32[1024]{0:T(1024)S(1)} %pad_clamp_fusion.2), kind=kCustom, calls=%fused_computation.clone.1 | custom fusion | bytes 2097216 | tf_op jit(solution)/shard_map/while/body/eval_jaxpr/gather | solution.py:21
  135.4 1.9 fusion.33
  137.4 0.6 gather_fusion
  138.1 1.4 fusion.32
  139.5 1.8 copy.39
  141.4 2.5 %gather_fusion.1 = bf16[16,2,128,128]{3,2,1,0:T(8,128)(2,1)S(1)} fusion(bf16[32,2,128,128]{3,2,1,0:T(8,128)(2,1)} %get-tuple-element.163, s32[1024]{0:T(1024)S(1)} %pad_clamp_fusion.2), kind=kCustom, calls=%fused_computation.clone.1 | custom fusion | bytes 2097216 | tf_op jit(solution)/shard_map/while/body/eval_jaxpr/gather | solution.py:21
  143.9 1.9 fusion.33
  145.8 0.6 gather_fusion
  146.4 0.1 copy.38
  146.5 1.4 fusion.32
  147.9 1.8 copy.39
  149.8 2.5 %gather_fusion.1 = bf16[16,2,128,128]{3,2,1,0:T(8,128)(2,1)S(1)} fusion(bf16[32,2,128,128]{3,2,1,0:T(8,128)(2,1)} %get-tuple-element.163, s32[1024]{0:T(1024)S(1)} %pad_clamp_fusion.2), kind=kCustom, calls=%fused_computation.clone.1 | custom fusion | bytes 2097216 | tf_op jit(solution)/shard_map/while/body/eval_jaxpr/gather | solution.py:21
  152.3 1.9 fusion.33
  154.2 0.6 gather_fusion
  154.8 0.1 copy.38
  154.9 1.4 fusion.32
  156.3 1.8 copy.39
  158.2 2.5 %gather_fusion.1 = bf16[16,2,128,128]{3,2,1,0:T(8,128)(2,1)S(1)} fusion(bf16[32,2,128,128]{3,2,1,0:T(8,128)(2,1)} %get-tuple-element.163, s32[1024]{0:T(1024)S(1)} %pad_clamp_fusion.2), kind=kCustom, calls=%fused_computation.clone.1 | custom fusion | bytes 2097216 | tf_op jit(solution)/shard_map/while/body/eval_jaxpr/gather | solution.py:21
  160.7 1.9 fusion.33
  162.6 0.3 copy.31
  162.8 0.8 bitcast_reduce_fusion
  163.7 0.6 reduce_sum.18
  164.3 39.5 %psum.7 = f32[]{:T(128)} all-reduce(f32[]{:T(128)} %reduce_sum.18), channel_id=1, replica_groups=mesh['row'=4,'col'=8] {'row','col'}, use_global_device_ids=true, to_apply=%region_5.6 | all-reduce | flops 1 | bytes 8 | tf_op jit(solution)/shard_map/psum | solution.py:62
  204.5 0.8 reshape_bitcast_fusion
  205.2 0.1 copy.32
  205.4 0.6 broadcast_multiply_fusion
  (68 shorter events, 1.0 us)
Async XLA Ops:
  7.2 12.3 %copy-start.1 = (s32[8,1,1,2]{0,3,2,1:T(2,128)S(1)}, s32[8,1,1,2]{0,3,2,1:T(2,128)}, u32[]{:S(2)}) copy-start(s32[8,1,1,2]{0,3,2,1:T(2,128)} %param.5) | copy-start | bytes 196
  7.2 50.8 %all-gather.3.cloned.1.call-start = ((), (), s32[]{:S(2)}) async-start(), calls=%async_computation.2 | async-start | bytes 2621440 | tf_op jit(solution)/shard_map/all_gather | solution.py:40
  7.9 87.4 %all-gather.5.cloned.1.call-start = ((), (), s32[]{:S(2)}) async-start(), calls=%async_computation.3 | async-start | bytes 4718592 | tf_op jit(solution)/shard_map/all_gather | solution.py:13
  9.9 18.5 %all-to-all-start = ((s32[4,8,1,1,2]{1,4,3,2,0:T(2,128)}), s32[4,8,1,1,2]{1,4,3,2,0:T(2,128)S(1)}, u32[]{:S(2)}, u32[]{:S(2)}) async-start(s32[4,8,1,1,2]{1,4,3,2,0:T(2,128)} %stack.2), calls=%async_computation | async-start | bytes 8192 | tf_op jit(solution)/shard_map/all_to_all | solution.py:39
  16.3 188.2 %reduce-scatter.4.cloned.1.call-start = ((), (), s32[]{:S(2)}) async-start(), calls=%async_computation.4 | async-start | bytes 73728
  99.3 2.5 %copy-start = (f32[16,2,128,128]{2,3,1,0:T(8,128)S(1)}, f32[16,2,128,128]{2,3,1,0:T(8,128)}, u32[]{:S(2)}) copy-start(f32[16,2,128,128]{2,3,1,0:T(8,128)} %copy.39) | copy-start | bytes 6291460 | tf_op jit(solution)/shard_map/while
  107.7 2.5 %copy-start = (f32[16,2,128,128]{2,3,1,0:T(8,128)S(1)}, f32[16,2,128,128]{2,3,1,0:T(8,128)}, u32[]{:S(2)}) copy-start(f32[16,2,128,128]{2,3,1,0:T(8,128)} %copy.39) | copy-start | bytes 6291460 | tf_op jit(solution)/shard_map/while
  116.1 2.5 %copy-start = (f32[16,2,128,128]{2,3,1,0:T(8,128)S(1)}, f32[16,2,128,128]{2,3,1,0:T(8,128)}, u32[]{:S(2)}) copy-start(f32[16,2,128,128]{2,3,1,0:T(8,128)} %copy.39) | copy-start | bytes 6291460 | tf_op jit(solution)/shard_map/while
  124.5 2.5 %copy-start = (f32[16,2,128,128]{2,3,1,0:T(8,128)S(1)}, f32[16,2,128,128]{2,3,1,0:T(8,128)}, u32[]{:S(2)}) copy-start(f32[16,2,128,128]{2,3,1,0:T(8,128)} %copy.39) | copy-start | bytes 6291460 | tf_op jit(solution)/shard_map/while
  132.9 2.5 %copy-start = (f32[16,2,128,128]{2,3,1,0:T(8,128)S(1)}, f32[16,2,128,128]{2,3,1,0:T(8,128)}, u32[]{:S(2)}) copy-start(f32[16,2,128,128]{2,3,1,0:T(8,128)} %copy.39) | copy-start | bytes 6291460 | tf_op jit(solution)/shard_map/while
  141.3 2.5 %copy-start = (f32[16,2,128,128]{2,3,1,0:T(8,128)S(1)}, f32[16,2,128,128]{2,3,1,0:T(8,128)}, u32[]{:S(2)}) copy-start(f32[16,2,128,128]{2,3,1,0:T(8,128)} %copy.39) | copy-start | bytes 6291460 | tf_op jit(solution)/shard_map/while
  149.8 2.5 %copy-start = (f32[16,2,128,128]{2,3,1,0:T(8,128)S(1)}, f32[16,2,128,128]{2,3,1,0:T(8,128)}, u32[]{:S(2)}) copy-start(f32[16,2,128,128]{2,3,1,0:T(8,128)} %copy.39) | copy-start | bytes 6291460 | tf_op jit(solution)/shard_map/while
  158.2 2.5 %copy-start = (f32[16,2,128,128]{2,3,1,0:T(8,128)S(1)}, f32[16,2,128,128]{2,3,1,0:T(8,128)}, u32[]{:S(2)}) copy-start(f32[16,2,128,128]{2,3,1,0:T(8,128)} %copy.39) | copy-start | bytes 6291460 | tf_op jit(solution)/shard_map/while
Sparse Core Ops, SparseCore 0:
  9.6 48.3 all-gather.2
  59.9 35.3 all-gather.4
  163.8 33.5 reduce-scatter.3
